TPU v7x, 32 devices: a whole 2x2x4 slice. The times are simulated.
32 devices in a mesh: grp: 4 (over z), head: 8 (over y, x, core).
Axes of the slice: x: 2, y: 2, z: 4, core: 2. Of those that a mesh axis runs over, the one named last changes fastest.
Arguments:
- inputs: bfloat16 [4, 64, 4096], P(None, 'grp', 'head'), parts along dimension 1, may hold values from -6 to 6
- gains: float32 [2, 4096], replicated, may hold values from 0.5 to 1.5
- decays: float32 [2, 32], P(None, 'head'), may hold values from 0.7 to 0.999
- w_qkv: bfloat16 [2, 4096, 3, 32, 128], P(None, None, None, 'head'), may hold values from -0.09375 to 0.09375
- w_out: bfloat16 [2, 32, 128, 4096], P(None, 'head'), may hold values from -0.125 to 0.125
- s_state: float32 [2, 64, 32, 128, 128], P(None, 'grp', 'head'), parts along dimension 1, may hold values from -0.5 to 0.5
- r_state: float32 [2, 64, 32, 128, 128], P(None, 'grp', 'head'), parts along dimension 1, as said below
Outputs:
- stream_out: float32 [4, 64, 4096], P(None, 'grp', 'head'), parts along dimension 1
- s_final: float32 [2, 64, 32, 128, 128], P(None, 'grp', 'head'), parts along dimension 1
- r_final: float32 [2, 64, 32, 128, 128], P(None, 'grp', 'head'), parts along dimension 1
There are 4 independent parts, one for each index of `grp`. A program takes and returns all parts, laid end to end along the dimension named above; an argument that names none is the same for every part. Nothing has to cross between parts.
Inputs may be any that keep to these rules, and one draw needn't show every extreme that they name: `r_state`: each matrix is symmetric positive definite with eigenvalues of 0.5 or more and of order one.
All inputs are finite; a program needn't handle non-finite values.
Results may differ from a plain program's by a relative error of at most 0.02.
Values may be sent and summed in bfloat16 or wider, within the bound.
A program may use at most 192 MiB of HBM per device.

v0:
```python
import functools

import jax
import jax.numpy as jnp
from jax import lax
from jax.experimental import pallas as pl
from jax.experimental.pallas import tpu as pltpu
from jax.sharding import PartitionSpec as P

EPSILON = 1e-05
RING = 4
CHUNK = 256
F32 = jnp.float32
BF16 = jnp.bfloat16
MESH = pl.DeviceIdType.MESH


def front_kernel(
    n, tokens, batch, heads, layers,
    x_ref, gains_ref, dec_ref, w_hbm, wo_hbm, s_hbm, r_hbm,
    y_ref, sv, rv,
    left_ref, right_ref, raw, wide, rep, wo, xg, lhs, acc, part, recv, cur, kq, pz, os, oo,
    raw_sem, in_sem, send_sem, recv_sem, own_sem,
):
    me = lax.axis_index("head")
    rows = tokens * batch
    hd = kq.shape[-1]
    width = lhs.shape[1]
    shard = x_ref.shape[1]
    mixed = 3 * heads
    chunks = width // CHUNK
    span = CHUNK * mixed

    def raw_copy(layer, c, slot):
        return pltpu.make_async_copy(
            w_hbm.at[layer, pl.ds(pl.multiple_of(c * span, span), span)],
            raw.at[slot],
            raw_sem.at[slot],
        )

    def state_copies(layer):
        return (
            pltpu.make_async_copy(r_hbm.at[layer], rv.at[layer], in_sem.at[0, layer]),
            pltpu.make_async_copy(s_hbm.at[layer], sv.at[layer], in_sem.at[1, layer]),
            pltpu.make_async_copy(wo_hbm.at[layer], wo.at[layer], in_sem.at[2, layer]),
        )

    def fill(layer):
        for c in range(min(RING, chunks)):
            raw_copy(layer, c, c).start()

    def repack(layer):
        def body(c, carry):
            slot = lax.rem(c, RING)
            raw_copy(layer, c, slot).wait()
            wide[...] = raw[slot].astype(F32)

            @pl.when(c + RING < chunks)
            def _():
                raw_copy(layer, c + RING, slot).start()

            base = pl.multiple_of(c * CHUNK, CHUNK)
            for m in range(mixed):
                rep[pl.ds(base, CHUNK), m * hd : (m + 1) * hd] = wide[
                    pl.ds(m, CHUNK, stride=mixed), :
                ].astype(BF16)
            return carry

        lax.fori_loop(0, chunks, body, 0)

    def send(src, dst, phase, peer):
        return pltpu.make_async_remote_copy(
            src_ref=src,
            dst_ref=dst,
            send_sem=send_sem.at[phase, peer],
            recv_sem=recv_sem.at[phase, me],
            device_id={"head": peer},
            device_id_type=MESH,
        )

    def peer_at(k):
        return lax.rem(me + k, n)

    def arrive(buf, phase, src):
        pltpu.make_async_copy(buf.at[src], buf.at[src], recv_sem.at[phase, src]).wait()

    fill(0)

    barrier = pltpu.get_barrier_semaphore()
    for k in range(1, n):
        pl.semaphore_signal(
            barrier, inc=1, device_id={"head": peer_at(k)}, device_id_type=MESH
        )
    pl.semaphore_wait(barrier, n - 1)

    def gather_start(layer, src):
        for k in range(1, n):
            send(src, xg.at[layer, me], 2 * layer, peer_at(k)).start()
        pltpu.make_async_copy(src, xg.at[layer, me], own_sem.at[0]).start()

    def gather_wait(layer, src):
        for k in range(1, n):
            arrive(xg.at[layer], 2 * layer, peer_at(k))
        pltpu.make_async_copy(src, xg.at[layer, me], own_sem.at[0]).wait()

    def project(layer):
        total = jnp.zeros((rows, 1), F32)
        for i in range(n):
            block = xg[layer, i].astype(F32)
            total = total + jnp.sum(block * block, axis=-1, keepdims=True)
            gain = gains_ref[layer, :, i * shard : (i + 1) * shard]
            lhs[:, i * shard : (i + 1) * shard] = (block * gain).astype(BF16)
        for at in range(0, mixed * hd, 2 * hd):
            stop = min(at + 2 * hd, mixed * hd)
            acc[:, at:stop] = jnp.dot(
                lhs[...], rep[:, at:stop], preferred_element_type=F32
            )
        return lax.rsqrt(total / width + EPSILON)

    def norm(v):
        return v * lax.rsqrt(jnp.mean(v * v, axis=-1, keepdims=True) + EPSILON)

    def dots(a, b):
        return jnp.sum(a * b, axis=-1, keepdims=True)

    def tok(t):
        return slice(t * batch, (t + 1) * batch)

    def per_pair(fn):
        step = 4 if batch % 4 == 0 else 1

        def body(i, carry):
            for j in range(step):
                b = i * step + j
                for h in range(heads):
                    fn(b, h)
            return carry

        lax.fori_loop(0, batch // step, body, 0)

    def mesa(layer, factor):
        copies = state_copies(layer)
        for h in range(heads):
            cols = [slice((j * heads + h) * hd, (j * heads + h + 1) * hd) for j in range(3)]
            kq[h, rows:, :] = norm(acc[:, cols[0]] * factor)
            kq[h, :rows, :] = norm(acc[:, cols[1]] * factor) * hd ** (-0.5)
            left_ref[layer, h, rows:, :] = acc[:, cols[2]] * factor
        copies[0].wait()

        def first(b, h):
            pair = kq[h, pl.ds(b, 2 * tokens, stride=batch), :].astype(BF16)
            pz[h, pl.ds(b, 2 * tokens, stride=batch), :] = jnp.dot(
                pair, rv[layer, b, h].astype(BF16), preferred_element_type=F32
            )

        per_pair(first)
        for h in range(heads):
            g = jnp.full((batch, 1), dec_ref[layer, h], F32)
            ginv = 1.0 / g
            ks = [kq[h, tok(t), :] for t in range(tokens)]
            qs = [kq[h, tok(tokens + t), :] for t in range(tokens)]
            ps = [pz[h, tok(t), :] for t in range(tokens)]
            zs = [pz[h, tok(tokens + t), :] for t in range(tokens)]
            back = [None] * (tokens + 1)
            front = [None] * (tokens + 1)
            back[0] = front[0] = jnp.ones_like(g)
            for t in range(tokens):
                back[t + 1] = back[t] * ginv
                front[t + 1] = front[t] * g
            for t in range(tokens):
                u = ps[t]
                inv = 1.0 / (g + dots(ks[t], u))
                for s in range(t + 1, tokens):
                    ps[s] = (ps[s] - u * (dots(u, ks[s]) * inv)) * ginv
                for s in range(t, tokens):
                    zs[s] = (zs[s] - u * (dots(u, qs[s]) * inv)) * ginv
                left_ref[layer, h, tok(t), :] = u
                right_ref[layer, h, tok(t), :] = u * (-inv * back[tokens - t])
                right_ref[layer, h, tok(tokens + t), :] = ks[t] * front[tokens - 1 - t]
                pz[h, tok(t), :] = zs[t]
        copies[1].wait()

        def second(b, h):
            pair = pz[h, pl.ds(b, 2 * tokens, stride=batch), :].astype(BF16)
            os[h, pl.ds(b, 2 * tokens, stride=batch), :] = lax.dot_general(
                pair, sv[layer, b, h].astype(BF16), (((1,), (1,)), ((), ())),
                preferred_element_type=F32,
            )

        per_pair(second)
        for h in range(heads):
            g = jnp.full((batch, 1), dec_ref[layer, h], F32)
            front = [jnp.ones_like(g)]
            for t in range(tokens):
                front.append(front[-1] * g)
            for t in range(tokens):
                w = pz[h, tok(t), :]
                out = os[h, tok(t), :] * front[t + 1]
                for s in range(t + 1):
                    v = left_ref[layer, h, tok(tokens + s), :]
                    out = out + v * (dots(kq[h, tok(s), :], w) * front[t - s])
                oo[tok(t), h * hd : (h + 1) * hd] = out.astype(BF16)
        copies[2].wait()

    def update(layer):
        upper = lax.broadcasted_iota(jnp.int32, (2 * tokens, hd), 0) < tokens
        scales = []
        for h in range(heads):
            g = jnp.full((1, hd), dec_ref[layer, h], F32)
            power = g
            for _ in range(tokens - 1):
                power = power * g
            scales.append((power, 1.0 / power))

        def pair(b, h):
            near = pl.ds(b, 2 * tokens, stride=batch)
            left = left_ref[layer, h, near, :]
            right = right_ref[layer, h, near, :]
            zero = jnp.zeros_like(right)
            both = jnp.concatenate(
                [jnp.where(upper, right, zero), jnp.where(upper, zero, right)], axis=1
            ).astype(BF16)
            change = jnp.dot(left.T.astype(BF16), both, preferred_element_type=F32)
            rv[layer, b, h] = rv[layer, b, h] * scales[h][1] + change[:, :hd]
            sv[layer, b, h] = sv[layer, b, h] * scales[h][0] + change[:, hd:]

        per_pair(pair)

    def mix(layer):
        phase = 2 * layer + 1
        for k in list(range(1, n)):
            p = peer_at(k)
            col = pl.ds(pl.multiple_of(p * shard, shard), shard)
            part[layer, p] = jnp.dot(
                oo[...], wo[layer, :, col], preferred_element_type=F32
            ).astype(BF16)
            send(part.at[layer, p], recv.at[layer, me], phase, p).start()
        col = pl.ds(pl.multiple_of(me * shard, shard), shard)
        return jnp.dot(oo[...], wo[layer, :, col], preferred_element_type=F32)

    def collect(layer):
        total = cur[...]
        for k in range(1, n):
            p = peer_at(k)
            arrive(recv.at[layer], 2 * layer + 1, p)
            total = total + recv[layer, p].astype(F32)
        return total

    gather_start(0, x_ref)
    repack(0)
    for layer in range(layers):
        for copy in state_copies(layer):
            copy.start()
    if layers > 1:
        fill(1)
    cur[...] = x_ref[...].astype(F32)
    gather_wait(0, x_ref)
    for layer in range(layers):
        factor = project(layer)
        mesa(layer, factor)
        cur[...] = cur[...] + mix(layer)
        if layer + 1 < layers:
            repack(layer + 1)
            if layer + 2 < layers:
                fill(layer + 2)
            total = collect(layer)
            cur[...] = total
            xg[layer + 1, me] = total.astype(BF16)
            for k in range(1, n):
                send(
                    xg.at[layer + 1, me], xg.at[layer + 1, me], 2 * layer + 2, peer_at(k)
                ).start()
            update(layer)
            for k in range(1, n):
                arrive(xg.at[layer + 1], 2 * layer + 2, peer_at(k))
        else:
            update(layer)
            y_ref[...] = collect(layer)
    for layer in range(layers):
        for k in range(1, n):
            p = peer_at(k)
            send(x_ref, xg.at[layer, me], 2 * layer, p).wait_send()
            send(part.at[layer, p], recv.at[layer, me], 2 * layer + 1, p).wait_send()


def on_device(n, inputs, gains, decays, w_qkv, w_out, s_state, r_state):
    layers, width, _, heads, hd = w_qkv.shape
    tokens, batch, shard = inputs.shape
    rows = tokens * batch
    mixed = 3 * heads
    vmem = pl.BlockSpec(memory_space=pltpu.VMEM)
    smem = pl.BlockSpec(memory_space=pltpu.SMEM)
    anywhere = pl.BlockSpec(memory_space=pl.ANY)
    pairs = (layers, heads, 2 * rows, hd)
    y, s_new, r_new = pl.pallas_call(
        functools.partial(front_kernel, n, tokens, batch, heads, layers),
        out_shape=(
            pltpu.VMEM((rows, shard), F32),
            pltpu.VMEM(s_state.shape, F32),
            pltpu.VMEM(r_state.shape, F32),
        ),
        in_specs=[vmem, vmem, smem, anywhere, anywhere, anywhere, anywhere],
        out_specs=(vmem, vmem, vmem),
        scratch_shapes=[
            pltpu.VMEM(pairs, F32),
            pltpu.VMEM(pairs, F32),
            pltpu.VMEM((RING, CHUNK * mixed, hd), BF16),
            pltpu.VMEM((CHUNK * mixed, hd), F32),
            pltpu.VMEM((width, mixed * hd), BF16),
            pltpu.VMEM((layers, heads * hd, width), BF16),
            pltpu.VMEM((layers, n, rows, shard), BF16),
            pltpu.VMEM((rows, width), BF16),
            pltpu.VMEM((rows, mixed * hd), F32),
            pltpu.VMEM((layers, n, rows, shard), BF16),
            pltpu.VMEM((layers, n, rows, shard), BF16),
            pltpu.VMEM((rows, shard), F32),
            pltpu.VMEM((heads, 2 * rows, hd), F32),
            pltpu.VMEM((heads, 2 * rows, hd), F32),
            pltpu.VMEM((heads, 2 * rows, hd), F32),
            pltpu.VMEM((rows, heads * hd), BF16),
            pltpu.SemaphoreType.DMA((RING,)),
            pltpu.SemaphoreType.DMA((3, layers)),
            pltpu.SemaphoreType.DMA((2 * layers, n)),
            pltpu.SemaphoreType.DMA((2 * layers, n)),
            pltpu.SemaphoreType.DMA((1,)),
        ],
        compiler_params=pltpu.CompilerParams(
            collective_id=0, has_side_effects=True, vmem_limit_bytes=42 * 1024 * 1024
        ),
        name="front",
    )(
        inputs.reshape(rows, shard),
        gains.reshape(layers, 1, width),
        decays,
        w_qkv.reshape(layers, width * mixed, hd),
        w_out.reshape(layers, heads * hd, width),
        s_state,
        r_state,
    )
    return y.reshape(tokens, batch, shard), s_new, r_new


def solution(mesh):
    in_specs = (
        P(None, "grp", "head"),
        P(),
        P(None, "head"),
        P(None, None, None, "head", None),
        P(None, "head", None, None),
        P(None, "grp", "head", None, None),
        P(None, "grp", "head", None, None),
    )
    out_specs = (
        P(None, "grp", "head"),
        P(None, "grp", "head", None, None),
        P(None, "grp", "head", None, None),
    )
    return jax.shard_map(
        functools.partial(on_device, mesh.shape["head"]),
        mesh=mesh,
        in_specs=in_specs,
        out_specs=out_specs,
        check_vma=False,
    )
```

profile of v0, /device:TPU:0, one launch (start us, length us, event | category | flops | bytes accessed | tf_op | source)
XLA Modules:
  0.0 55.2 jit_solution(7271887168276777368)
XLA Ops:
  0.6 1.4 %reshape.22.gains_ref = f32[2,1,4096]{2,1,0:T(1,128)} reshape(f32[2,4096]{1,0:T(2,128)} %param.8) | data formatting | bytes 65536 | tf_op jit(solution)/shard_map/reshape | solution.py:333
  2.0 45.7 %front.1 = (f32[64,512]{1,0:T(8,128)S(1)}, f32[2,16,4,128,128]{4,3,2,1,0:T(8,128)S(1)}, f32[2,16,4,128,128]{4,3,2,1,0:T(8,128)S(1)}) custom-call(bf16[64,512]{1,0:T(8,128)(2,1)} %bitcast.7, f32[2,1,4096]{2,1,0:T(1,128)} %reshape.22.gains_ref, f32[2,4]{1,0:T(2,128)} %dec_ref.1, bf16[2,49152,128]{2,1,0:T(8,128)(2,1)} %bitcast.5, ...), custom_call_target="tpu_custom_call" | custom-call | tf_op jit(solution)/shard_map/front/pallas_call | solution.py:295
  47.7 0.7 %copy.13 = f32[4,16,512]{2,1,0:T(8,128)} copy(f32[4,16,512]{2,1,0:T(8,128)S(1)} %bitcast.4) | data formatting | bytes 262144
  48.4 3.4 %copy.14 = f32[2,16,4,128,128]{4,3,2,1,0:T(8,128)} copy(f32[2,16,4,128,128]{4,3,2,1,0:T(8,128)S(1)} %get-tuple-element.10) | data formatting | bytes 16777216
  51.8 3.4 %copy.15 = f32[2,16,4,128,128]{4,3,2,1,0:T(8,128)} copy(f32[2,16,4,128,128]{4,3,2,1,0:T(8,128)S(1)} %get-tuple-element.11) | data formatting | bytes 16777216
where the time goes:
time: 56.2 us; the launch traced here: 55.2 us
  Pallas kernels  45.7 us (81%)
  local copies, waits for them, and re-layouts  8.85 us (16%)
  between operations  0.64 us (1%)
    pallas_call x1, Pallas kernels, on_device(): pl.pallas_call(functools.partial(front_kernel, n, tokens, batch, heads, l...  45.7 us
    unnamed x3, local copies, waits for them, and re-layouts  7.45 us
    reshape x1, local copies, waits for them, and re-layouts, on_device(): gains.reshape(layers, 1, width)  1.4 us

commit v1 on v0

v1 whole, which is shorter than its diff:
```python
import functools

import jax
import jax.numpy as jnp
from jax import lax
from jax.experimental import pallas as pl
from jax.experimental.pallas import tpu as pltpu
from jax.sharding import PartitionSpec as P

EPSILON = 1e-05
PIECES = 4
PARTS = 1
F32 = jnp.float32
BF16 = jnp.bfloat16
MESH = pl.DeviceIdType.MESH


def front_kernel(
    n, tokens, batch, heads, layers, parts,
    x_hbm, gains_hbm, dec_hbm, w_hbm, wo_hbm, s_hbm, r_hbm,
    y_ref, sv, rv,
    xin, gains_ref, dec_ref, w, wo, spread, xg, lhs, acc, squares, near, far, pair, recv, mine, cur,
    kq, pz, os, oo, left_ref, right_ref,
    misc_sem, w_sem, wo_sem, state_sem, ag_send, ag_recv, sib_send, sib_recv, rs_send, rs_recv,
):
    me = lax.axis_index("head")
    side = lax.rem(me, 2)
    chip = me // 2
    chips = n // 2
    sibling = me + 1 - 2 * side
    hd = kq.shape[-1]
    width = gains_ref.shape[1]
    shard = xin.shape[2]
    span = batch // parts
    rows = tokens * span
    mixed = 3 * heads
    pack = lhs.shape[1] // rows
    groups = mixed // pack
    piece = width // PIECES

    def w_copies(layer):
        out = []
        for c in range(PIECES):
            at = pl.ds(c * piece, piece)
            if pack == 1:
                out.append(
                    pltpu.make_async_copy(
                        w_hbm.at[layer, at], w.at[layer, at], w_sem.at[layer, c]
                    )
                )
                continue
            octs = pl.ds(c * piece // 8, piece // 8)
            for s in range(8):
                out.append(
                    pltpu.make_async_copy(
                        w_hbm.at[layer, octs, s],
                        w.at[layer, octs, :, pl.ds(s * pack, pack)],
                        w_sem.at[layer, c],
                    )
                )
        return out

    def w_wait(layer):
        for c in range(PIECES):
            at = pl.ds(c * piece // (8 if pack > 1 else 1), piece // (8 if pack > 1 else 1))
            pltpu.make_async_copy(w.at[layer, at], w.at[layer, at], w_sem.at[layer, c]).wait()

    def wo_copy(layer):
        return pltpu.make_async_copy(wo_hbm.at[layer], wo.at[layer], wo_sem.at[layer])

    def state_copy(which, layer, part):
        src, dst = ((r_hbm, rv), (s_hbm, sv))[which]
        at = pl.ds(part * span, span)
        return pltpu.make_async_copy(
            src.at[layer, at], dst.at[layer, at], state_sem.at[which, layer, part]
        )

    started = []

    def send(src, dst, out_sem, in_sem, peer):
        copy = pltpu.make_async_remote_copy(
            src_ref=src,
            dst_ref=dst,
            send_sem=out_sem,
            recv_sem=in_sem,
            device_id={"head": peer},
            device_id_type=MESH,
        )
        copy.start()
        started.append(copy)

    def arrive(buf, sem):
        pltpu.make_async_copy(buf, buf, sem).wait()

    def peer(k):
        return lax.rem(me + 2 * k, n)

    def block_at(k, other):
        at = 2 * lax.rem(chip - k + chips, chips)
        return at + (1 - side if other else side)

    misc = (
        pltpu.make_async_copy(x_hbm, xin, misc_sem.at[0]),
        pltpu.make_async_copy(gains_hbm, gains_ref, misc_sem.at[1]),
        pltpu.make_async_copy(dec_hbm, dec_ref, misc_sem.at[2]),
    )
    for copy in misc:
        copy.start()
    barrier = pltpu.get_barrier_semaphore()
    for k in range(1, chips):
        pl.semaphore_signal(barrier, inc=1, device_id={"head": peer(k)}, device_id_type=MESH)
    pl.semaphore_signal(barrier, inc=1, device_id={"head": sibling}, device_id_type=MESH)
    for copy in w_copies(0):
        copy.start()
    for part in range(parts):
        state_copy(0, 0, part).start()
    if pack > 1:
        row = lax.broadcasted_iota(jnp.int32, spread.shape, 0)
        col = lax.broadcasted_iota(jnp.int32, spread.shape, 1)
        half = spread.shape[1] // 2
        hit = jnp.where(col < half, col - 2 * row, col - half - 2 * row - 1)
        spread[...] = jnp.where(hit == 0, 1.0, 0.0).astype(BF16)
    misc[0].wait()
    whole = [xin[t].astype(F32) for t in range(tokens)]
    for part in range(parts):
        piece_x = jnp.concatenate([v[part * span : (part + 1) * span] for v in whole], axis=0)
        cur[part] = piece_x
        xg[0, part, 0, 0] = piece_x.astype(BF16)
    pl.semaphore_wait(barrier, chips)

    def gather_start(layer, part):
        own = xg.at[layer, part, 0, 0]
        for k in range(1, chips):
            send(
                own, xg.at[layer, part, k, 0],
                ag_send.at[layer, part, 0, k], ag_recv.at[layer, part, 0, k], peer(k),
            )
        send(
            own, xg.at[layer, part, 0, 1],
            ag_send.at[layer, part, 0, 0], ag_recv.at[layer, part, 1, 0], sibling,
        )

    def forward(layer, part):
        total = expand(layer, part, 0, 0)
        arrive(xg.at[layer, part, 0, 1], ag_recv.at[layer, part, 1, 0])
        total = total + expand(layer, part, 0, 1)
        for k in range(1, chips):
            arrive(xg.at[layer, part, k, 0], ag_recv.at[layer, part, 0, k])
            send(
                xg.at[layer, part, k, 0], xg.at[layer, part, k, 1],
                ag_send.at[layer, part, 1, k], ag_recv.at[layer, part, 1, k], sibling,
            )
        for k in range(1, chips):
            total = total + expand(layer, part, k, 0)
        squares[part] = total

    def expand(layer, part, k, other):
        i = block_at(k, other)
        block = xg[layer, part, k, other].astype(F32)
        gain = gains_ref[layer : layer + 1, pl.ds(pl.multiple_of(i * shard, shard), shard)]
        square = block * block
        total = square[:, :128]
        for at in range(128, shard, 128):
            total = total + square[:, at : at + 128]
        scaled = (block * gain).astype(BF16)
        slot = 2 * k + other
        if pack == 1:
            lhs[slot] = scaled
            return total
        wide = spread.shape[1] // 2
        stack = jnp.concatenate(
            [scaled[:, at : at + 128] for at in range(0, shard, 128)], axis=0
        )
        out = jnp.dot(stack, spread[...], preferred_element_type=F32).astype(BF16)
        for s in range(shard // 128):
            for p in range(pack):
                lhs[slot, p * rows : (p + 1) * rows, s * wide : (s + 1) * wide] = out[
                    s * rows : (s + 1) * rows, p * wide : (p + 1) * wide
                ]
        return total

    def multiply(layer, part, slots, first):
        for g in range(0, groups, 2):
            many = min(2, groups - g)
            total = None
            for k, other in slots:
                i = block_at(k, other)
                if pack == 1:
                    at = pl.ds(pl.multiple_of(i * shard, shard), shard)
                    weights = w[layer, at, g * hd : (g + many) * hd]
                else:
                    at = pl.ds(i * (shard // 8), shard // 8)
                    weights = jnp.concatenate(
                        [
                            w[layer, at, g + j].reshape(pack * shard, hd)
                            for j in range(many)
                        ],
                        axis=1,
                    )
                term = jnp.dot(lhs[2 * k + other], weights, preferred_element_type=F32)
                total = term if total is None else total + term
            cols = slice(g * hd, (g + many) * hd)
            acc[part, :, cols] = total if first else acc[part, :, cols] + total

    def project_near(layer, part):
        slots = [(k, 0) for k in range(chips)] + [(0, 1)]
        multiply(layer, part, slots, True)

    def project_far(layer, part):
        slots = [(k, 1) for k in range(1, chips)]
        total = squares[part]
        for k, other in slots:
            arrive(xg.at[layer, part, k, 1], ag_recv.at[layer, part, 1, k])
        for k, other in slots:
            total = total + expand(layer, part, k, other)
        multiply(layer, part, slots, False)
        return lax.rsqrt(jnp.sum(total, axis=-1, keepdims=True) / width + EPSILON)

    def norm(v):
        return v * lax.rsqrt(jnp.mean(v * v, axis=-1, keepdims=True) + EPSILON)

    def dots(a, b):
        return jnp.sum(a * b, axis=-1, keepdims=True)

    def tok(t):
        return slice(t * span, (t + 1) * span)

    def per_pair(fn):
        step = 4 if span % 4 == 0 else 1

        def body(i, carry):
            for j in range(step):
                b = i * step + j
                for h in range(heads):
                    fn(b, h)
            return carry

        lax.fori_loop(0, span // step, body, 0)

    def mesa(layer, part, factor):
        base = part * span

        def projected(j, h):
            at = j * heads + h
            p, g = at % pack, at // pack
            return acc[part, p * rows : (p + 1) * rows, g * hd : (g + 1) * hd] * factor

        for h in range(heads):
            kq[h, rows:, :] = norm(projected(0, h))
            kq[h, :rows, :] = norm(projected(1, h)) * hd ** (-0.5)
            left_ref[layer, part, h, rows:, :] = projected(2, h)
        state_copy(0, layer, part).wait()

        def first(b, h):
            both = kq[h, pl.ds(b, 2 * tokens, stride=span), :].astype(BF16)
            pz[h, pl.ds(b, 2 * tokens, stride=span), :] = jnp.dot(
                both, rv[layer, base + b, h].astype(BF16), preferred_element_type=F32
            )

        per_pair(first)
        for h in range(heads):
            g = jnp.full((span, 1), dec_ref[layer, h], F32)
            ginv = 1.0 / g
            ks = [kq[h, tok(t), :] for t in range(tokens)]
            qs = [kq[h, tok(tokens + t), :] for t in range(tokens)]
            ps = [pz[h, tok(t), :] for t in range(tokens)]
            zs = [pz[h, tok(tokens + t), :] for t in range(tokens)]
            back = [None] * (tokens + 1)
            front = [None] * (tokens + 1)
            back[0] = front[0] = jnp.ones_like(g)
            for t in range(tokens):
                back[t + 1] = back[t] * ginv
                front[t + 1] = front[t] * g
            for t in range(tokens):
                u = ps[t]
                inv = 1.0 / (g + dots(ks[t], u))
                for s in range(t + 1, tokens):
                    ps[s] = (ps[s] - u * (dots(u, ks[s]) * inv)) * ginv
                for s in range(t, tokens):
                    zs[s] = (zs[s] - u * (dots(u, qs[s]) * inv)) * ginv
                left_ref[layer, part, h, tok(t), :] = u
                right_ref[layer, part, h, tok(t), :] = u * (-inv * back[tokens - t])
                right_ref[layer, part, h, tok(tokens + t), :] = ks[t] * front[tokens - 1 - t]
                pz[h, tok(t), :] = zs[t]
        state_copy(1, layer, part).wait()

        def second(b, h):
            both = pz[h, pl.ds(b, 2 * tokens, stride=span), :].astype(BF16)
            os[h, pl.ds(b, 2 * tokens, stride=span), :] = lax.dot_general(
                both, sv[layer, base + b, h].astype(BF16), (((1,), (1,)), ((), ())),
                preferred_element_type=F32,
            )

        per_pair(second)
        for h in range(heads):
            g = jnp.full((span, 1), dec_ref[layer, h], F32)
            front = [jnp.ones_like(g)]
            for t in range(tokens):
                front.append(front[-1] * g)
            outs = []
            for t in range(tokens):
                z = pz[h, tok(t), :]
                out = os[h, tok(t), :] * front[t + 1]
                for s in range(t + 1):
                    v = left_ref[layer, part, h, tok(tokens + s), :]
                    out = out + v * (dots(kq[h, tok(s), :], z) * front[t - s])
                outs.append(out)
            oo[part, :, h * hd : (h + 1) * hd] = jnp.concatenate(outs, axis=0).astype(BF16)

    def update(layer, part):
        base = part * span
        upper = lax.broadcasted_iota(jnp.int32, (2 * tokens, hd), 0) < tokens
        scales = []
        for h in range(heads):
            g = jnp.full((1, hd), dec_ref[layer, h], F32)
            power = g
            for _ in range(tokens - 1):
                power = power * g
            scales.append((power, 1.0 / power))

        def change_of(b, h):
            at = pl.ds(b, 2 * tokens, stride=span)
            left = left_ref[layer, part, h, at, :]
            right = right_ref[layer, part, h, at, :]
            zero = jnp.zeros_like(right)
            both = jnp.concatenate(
                [jnp.where(upper, right, zero), jnp.where(upper, zero, right)], axis=1
            ).astype(BF16)
            change = jnp.dot(left.T.astype(BF16), both, preferred_element_type=F32)
            rv[layer, base + b, h] = rv[layer, base + b, h] * scales[h][1] + change[:, :hd]
            sv[layer, base + b, h] = sv[layer, base + b, h] * scales[h][0] + change[:, hd:]

        per_pair(change_of)

    def mix(layer, part):
        def product(k, other):
            i = 2 * lax.rem(chip + k, chips) + (1 - side if other else side)
            col = pl.ds(pl.multiple_of(i * shard, shard), shard)
            return jnp.dot(oo[part], wo[layer, :, col], preferred_element_type=F32)

        order = list(range(1, chips)) + [0]
        for k in order:
            near[layer, part, k] = product(k, 1).astype(BF16)
        for k in order:
            send(
                near.at[layer, part, k], far.at[layer, part, k],
                sib_send.at[layer, part, k], sib_recv.at[layer, part, k], sibling,
            )
        for k in order:
            mine[part, k] = product(k, 0)

    def scatter(layer, part):
        for k in range(1, chips):
            arrive(far.at[layer, part, k], sib_recv.at[layer, part, k])
            pair[layer, part, k] = (
                mine[part, k] + far[layer, part, k].astype(F32)
            ).astype(BF16)
            send(
                pair.at[layer, part, k], recv.at[layer, part, k],
                rs_send.at[layer, part, k], rs_recv.at[layer, part, k], peer(k),
            )

    def collect(layer, part):
        arrive(far.at[layer, part, 0], sib_recv.at[layer, part, 0])
        total = cur[part] + mine[part, 0] + far[layer, part, 0].astype(F32)
        for k in range(1, chips):
            arrive(recv.at[layer, part, k], rs_recv.at[layer, part, k])
            total = total + recv[layer, part, k].astype(F32)
        cur[part] = total
        if layer + 1 < layers:
            xg[layer + 1, part, 0, 0] = total.astype(BF16)
            gather_start(layer + 1, part)
        else:
            for t in range(tokens):
                y_ref[t, part * span : (part + 1) * span, :] = total[t * span : (t + 1) * span]

    every = range(parts)
    for part in every:
        gather_start(0, part)
    for copy in misc[1:]:
        copy.wait()
    for layer in range(layers):
        for part in every:
            if layer > 0 and part > 0:
                collect(layer - 1, part)
            forward(layer, part)
            if part == 0:
                w_wait(layer)
                if layer == 0:
                    for p in every:
                        state_copy(1, 0, p).start()
                    wo_copy(0).start()
            project_near(layer, part)
            if part > 0:
                scatter(layer, part - 1)
            if part == 0 and layer + 1 < layers:
                for copy in w_copies(layer + 1):
                    copy.start()
            factor = project_far(layer, part)
            mesa(layer, part, factor)
            if part == 0:
                wo_copy(layer).wait()
            mix(layer, part)
            if part == 0 and layer + 1 < layers:
                for which in range(2):
                    for p in every:
                        state_copy(which, layer + 1, p).start()
                wo_copy(layer + 1).start()
        scatter(layer, parts - 1)
        if layer + 1 < layers:
            collect(layer, 0)
            for part in every:
                update(layer, part)
        else:
            for part in every:
                if part + 1 < parts:
                    collect(layer, part)
                update(layer, part)
            collect(layer, parts - 1)
    for copy in started:
        copy.wait_send()


def back_kernel(y_vmem, s_vmem, r_vmem, y_hbm, s_hbm, r_hbm, sems):
    copies = [pltpu.make_async_copy(y_vmem, y_hbm, sems.at[2, 0, 0])]
    layers, count = s_vmem.shape[:2]
    cut = count // sems.shape[2]
    for layer in range(layers):
        for c in range(sems.shape[2]):
            at = pl.ds(c * cut, cut)
            copies.append(
                pltpu.make_async_copy(
                    s_vmem.at[layer, at], s_hbm.at[layer, at], sems.at[0, layer, c]
                )
            )
            copies.append(
                pltpu.make_async_copy(
                    r_vmem.at[layer, at], r_hbm.at[layer, at], sems.at[1, layer, c]
                )
            )
    for copy in copies:
        copy.start()
    for copy in copies:
        copy.wait()


def on_device(n, inputs, gains, decays, w_qkv, w_out, s_state, r_state):
    layers, width, _, heads, hd = w_qkv.shape
    tokens, batch, shard = inputs.shape
    parts = PARTS if batch % (8 * PARTS) == 0 else 1
    span = batch // parts
    rows = tokens * span
    mixed = 3 * heads
    pack = 2 if heads % 2 == 0 else 1
    groups = mixed // pack
    chips = n // 2
    vmem = pl.BlockSpec(memory_space=pltpu.VMEM)
    anywhere = pl.BlockSpec(memory_space=pl.ANY)
    if pack == 1:
        w_view = w_qkv.reshape(layers, width, mixed * hd)
        w_vmem = pltpu.VMEM(w_view.shape, BF16)
    else:
        w_view = w_qkv.reshape(layers, width // 8, 8, groups, pack, hd)
        w_vmem = pltpu.VMEM((layers, width // 8, groups, 8 * pack, hd), BF16)
    blocks = (layers, parts, chips, rows, shard)
    pairs = (layers, parts, heads, 2 * rows, hd)
    dma = pltpu.SemaphoreType.DMA
    y, s_new, r_new = pl.pallas_call(
        functools.partial(front_kernel, n, tokens, batch, heads, layers, parts),
        out_shape=(
            pltpu.VMEM(inputs.shape, F32),
            pltpu.VMEM(s_state.shape, F32),
            pltpu.VMEM(r_state.shape, F32),
        ),
        in_specs=[anywhere] * 7,
        out_specs=(vmem, vmem, vmem),
        scratch_shapes=[
            pltpu.VMEM(inputs.shape, BF16),
            pltpu.VMEM((layers, width), F32),
            pltpu.SMEM(decays.shape, F32),
            w_vmem,
            pltpu.VMEM((layers, heads * hd, width), BF16),
            pltpu.VMEM((128, 128 * pack * 2), BF16),
            pltpu.VMEM((layers, parts, chips, 2, rows, shard), BF16),
            pltpu.VMEM((n, pack * rows, pack * shard), BF16),
            pltpu.VMEM((parts, pack * rows, groups * hd), F32),
            pltpu.VMEM((parts, rows, 128), F32),
            pltpu.VMEM(blocks, BF16),
            pltpu.VMEM(blocks, BF16),
            pltpu.VMEM(blocks, BF16),
            pltpu.VMEM(blocks, BF16),
            pltpu.VMEM(blocks[1:], F32),
            pltpu.VMEM((parts, rows, shard), F32),
            pltpu.VMEM((heads, 2 * rows, hd), F32),
            pltpu.VMEM((heads, 2 * rows, hd), F32),
            pltpu.VMEM((heads, 2 * rows, hd), F32),
            pltpu.VMEM((parts, rows, heads * hd), BF16),
            pltpu.VMEM(pairs, F32),
            pltpu.VMEM(pairs, F32),
            dma((3,)),
            dma((layers, PIECES)),
            dma((layers,)),
            dma((2, layers, parts)),
            dma((layers, parts, 2, chips)),
            dma((layers, parts, 2, chips)),
            dma((layers, parts, chips)),
            dma((layers, parts, chips)),
            dma((layers, parts, chips)),
            dma((layers, parts, chips)),
        ],
        compiler_params=pltpu.CompilerParams(
            collective_id=0, has_side_effects=True, vmem_limit_bytes=44 * 1024 * 1024
        ),
        name="front",
    )(
        inputs,
        gains,
        decays,
        w_view,
        w_out.reshape(layers, heads * hd, width),
        s_state,
        r_state,
    )
    return pl.pallas_call(
        back_kernel,
        out_shape=tuple(
            jax.ShapeDtypeStruct(a.shape, F32) for a in (inputs, s_state, r_state)
        ),
        in_specs=[vmem] * 3,
        out_specs=(anywhere,) * 3,
        scratch_shapes=[dma((3, layers, 4))],
        compiler_params=pltpu.CompilerParams(vmem_limit_bytes=1024 * 1024),
        name="back",
    )(y, s_new, r_new)


def solution(mesh):
    in_specs = (
        P(None, "grp", "head"),
        P(),
        P(None, "head"),
        P(None, None, None, "head", None),
        P(None, "head", None, None),
        P(None, "grp", "head", None, None),
        P(None, "grp", "head", None, None),
    )
    out_specs = (
        P(None, "grp", "head"),
        P(None, "grp", "head", None, None),
        P(None, "grp", "head", None, None),
    )
    return jax.shard_map(
        functools.partial(on_device, mesh.shape["head"]),
        mesh=mesh,
        in_specs=in_specs,
        out_specs=out_specs,
        check_vma=False,
    )
```

time: 56.2 us -> 47.3 us (0.84); the launches traced: 55.2 us -> 47.1 us
  local copies, waits for them, and re-layouts: 8.85 us -> 0 us
  Pallas kernels: 45.7 us -> 46.5 us
    unnamed x3 -> x0, local copies, waits for them, and re-layouts: 7.45 us -> none
    pallas_call x0 -> x1, Pallas kernels: none -> 6.08 us  [on_device(): pl.pallas_call(back_kernel, out_shape=tuple((jax.ShapeDtypeStruct(a.shape...]
    pallas_call x1, Pallas kernels: 45.7 us -> 40.4 us  [on_device(): pl.pallas_call(functools.partial(front_kernel, n, tokens, batch, heads, l...]
    reshape x1 -> x0, local copies, waits for them, and re-layouts: 1.4 us -> none  [on_device(): gains.reshape(layers, 1, width)]
where the time goes in v1:
time: 47.3 us; the launch traced here: 47.1 us
  Pallas kernels  46.5 us (98%)
  between operations  0.64 us (1%)
    pallas_call x1, Pallas kernels, on_device(): pl.pallas_call(functools.partial(front_kernel, n, tokens, batch, heads, l...  40.4 us
    pallas_call x1, Pallas kernels, on_device(): pl.pallas_call(back_kernel, out_shape=tuple((jax.ShapeDtypeStruct(a.shape...  6.08 us

profile of v1, /device:TPU:0, one launch (start us, length us, event | category | flops | bytes accessed | tf_op | source)
XLA Modules:
  0.0 47.1 jit_solution(16770436789736985105)
XLA Ops:
  0.6 40.4 %front.1 = (f32[4,16,512]{2,1,0:T(8,128)S(1)}, f32[2,16,4,128,128]{4,3,2,1,0:T(8,128)S(1)}, f32[2,16,4,128,128]{4,3,2,1,0:T(8,128)S(1)}) custom-call(bf16[4,16,512]{2,1,0:T(8,128)(2,1)} %x_hbm.1, f32[2,4096]{1,0:T(2,128)} %gains_hbm.1, f32[2,4]{1,0:T(2,128)} %dec_hbm.1, bf16[2,512,8,6,2,128]{5,4,3,2,1,0:T(2,128)(2,1)} %bitcast.2, ...), custom_call_target="tpu_custom_call" | custom-call | tf_op jit(solution)/shard_map/front/pallas_call | solution.py:468
  41.0 6.1 %back.1 = (f32[4,16,512]{2,1,0:T(8,128)}, f32[2,16,4,128,128]{4,3,2,1,0:T(8,128)}, f32[2,16,4,128,128]{4,3,2,1,0:T(8,128)}) custom-call(f32[4,16,512]{2,1,0:T(8,128)S(1)} %get-tuple-element.6.y_vmem, f32[2,16,4,128,128]{4,3,2,1,0:T(8,128)S(1)} %get-tuple-element.7.s_vmem, f32[2,16,4,128,128]{4,3,2,1,0:T(8,128)S(1)} %get-tuple-element.8.r_vmem), custom_call_target="tpu_custom_call" | custom-call | tf_op jit(solution)/shard_map/back/pallas_call | solution.py:524

commit v2 on v1

v2 whole, which is shorter than its diff:
```python
import functools

import jax
import jax.numpy as jnp
from jax import lax
from jax.experimental import pallas as pl
from jax.experimental.pallas import tpu as pltpu
from jax.sharding import PartitionSpec as P

EPSILON = 1e-05
PARTS = 2
CUTS = 4
F32 = jnp.float32
BF16 = jnp.bfloat16
MESH = pl.DeviceIdType.MESH


def front_kernel(
    n, tokens, batch, heads, layers, parts,
    x_hbm, gains_hbm, dec_hbm, w_hbm, wo_hbm, s_hbm, r_hbm,
    y_ref, sv, rv,
    xin, gains_ref, dec_ref, w, wo, spread, xg, lhs, acc, squares, near, far, pair, recv, mine, cur,
    kq, pz, os, oo, left_ref, right_ref,
    misc_sem, w_sem, wo_sem, state_sem, out_sem, ag_recv, rs_recv,
):
    me = lax.axis_index("head")
    side = lax.rem(me, 2)
    chip = me // 2
    chips = n // 2
    sibling = me + 1 - 2 * side
    hd = kq.shape[-1]
    width = gains_ref.shape[1]
    shard = xin.shape[2]
    full = tokens * batch
    rows = full // parts
    mixed = 3 * heads
    pack = lhs.shape[1] // full
    groups = mixed // pack

    def w_rows(k):
        unit = 2 * shard // (8 if pack > 1 else 1)
        at = lax.rem(chip - k + chips, chips) * unit
        return pl.ds(pl.multiple_of(at, unit), unit)

    def w_copies(layer):
        out = []
        for k in range(chips):
            at, sem = w_rows(k), w_sem.at[layer, k]
            if pack == 1:
                out.append(pltpu.make_async_copy(w_hbm.at[layer, at], w.at[layer, at], sem))
                continue
            for s in range(8):
                out.append(
                    pltpu.make_async_copy(
                        w_hbm.at[layer, at, s],
                        w.at[layer, at, :, pl.ds(s * pack, pack)],
                        sem,
                    )
                )
        return out

    def w_wait(layer, k):
        part = w.at[layer, w_rows(k)]
        pltpu.make_async_copy(part, part, w_sem.at[layer, k]).wait()

    def wo_copy(layer):
        return pltpu.make_async_copy(wo_hbm.at[layer], wo.at[layer], wo_sem.at[layer])

    def state_copy(which, layer):
        src, dst = ((r_hbm, rv), (s_hbm, sv))[which]
        return pltpu.make_async_copy(src.at[layer], dst.at[layer], state_sem.at[which, layer])

    def send(layer, kind, src, dst, in_sem, peer):
        pltpu.make_async_remote_copy(
            src_ref=src,
            dst_ref=dst,
            send_sem=out_sem.at[layer, kind],
            recv_sem=in_sem,
            device_id={"head": peer},
            device_id_type=MESH,
        ).start()

    def settle(layer):
        some = pl.ds(1, chips - 1)
        sent = (
            xg.at[layer, :, 0],
            xg.at[layer, :, 0, some],
            near.at[layer],
            pair.at[layer, :, some],
        )
        for kind, blocks in enumerate(sent):
            pltpu.make_async_copy(blocks, blocks, out_sem.at[layer, kind]).wait()

    def arrive(buf, sem):
        pltpu.make_async_copy(buf, buf, sem).wait()

    def peer(k):
        return lax.rem(me + 2 * k, n)

    def block_at(k, other):
        at = 2 * lax.rem(chip - k + chips, chips)
        return at + (1 - side if other else side)

    misc = (
        pltpu.make_async_copy(x_hbm, xin, misc_sem.at[0]),
        pltpu.make_async_copy(gains_hbm, gains_ref, misc_sem.at[1]),
        pltpu.make_async_copy(dec_hbm, dec_ref, misc_sem.at[2]),
    )
    for copy in misc:
        copy.start()
    barrier = pltpu.get_barrier_semaphore()
    for k in range(1, chips):
        pl.semaphore_signal(barrier, inc=1, device_id={"head": peer(k)}, device_id_type=MESH)
    pl.semaphore_signal(barrier, inc=1, device_id={"head": sibling}, device_id_type=MESH)
    for copy in w_copies(0):
        copy.start()
    if pack > 1:
        row = lax.broadcasted_iota(jnp.int32, spread.shape, 0)
        col = lax.broadcasted_iota(jnp.int32, spread.shape, 1)
        half = spread.shape[1] // 2
        hit = jnp.where(col < half, col - 2 * row, col - half - 2 * row - 1)
        spread[...] = jnp.where(hit == 0, 1.0, 0.0).astype(BF16)
    misc[0].wait()
    start = jnp.concatenate([xin[t] for t in range(tokens)], axis=0)
    for part in range(parts):
        rows_x = start[part * rows : (part + 1) * rows]
        cur[part] = rows_x.astype(F32)
        xg[0, part, 0, 0] = rows_x
    pl.semaphore_wait(barrier, chips)

    def gather_start(layer, part):
        own = xg.at[layer, part, 0, 0]
        for k in range(1, chips):
            send(layer, 0, own, xg.at[layer, part, 0, k], ag_recv.at[0, layer, part], peer(k))
        send(layer, 0, own, xg.at[layer, part, 1, 0], ag_recv.at[1, layer, part], sibling)

    def forward(layer, part):
        arrive(xg.at[layer, part, 0, pl.ds(1, chips - 1)], ag_recv.at[0, layer, part])
        for k in range(1, chips):
            send(
                layer, 1, xg.at[layer, part, 0, k], xg.at[layer, part, 1, k],
                ag_recv.at[2, layer, part], sibling,
            )

    def forwarded(layer, part):
        arrive(xg.at[layer, part, 1, pl.ds(1, chips - 1)], ag_recv.at[2, layer, part])

    def expand(layer, slots, which):
        stack = []
        for k, other in slots:
            i = block_at(k, other)
            gain = gains_ref[layer : layer + 1, pl.ds(pl.multiple_of(i * shard, shard), shard)]
            for part in which:
                block = xg[layer, part, other, k].astype(F32)
                square = block * block
                total = square[:, :128]
                for at in range(128, shard, 128):
                    total = total + square[:, at : at + 128]
                squares[part] = squares[part] + total
                scaled = (block * gain).astype(BF16)
                if pack == 1:
                    lhs[2 * k + other, part * rows : (part + 1) * rows] = scaled
                else:
                    stack += [scaled[:, at : at + 128] for at in range(0, shard, 128)]
        if pack == 1:
            return
        wide = spread.shape[1] // 2
        out = jnp.dot(
            jnp.concatenate(stack, axis=0), spread[...], preferred_element_type=F32
        ).astype(BF16)
        at = 0
        for k, other in slots:
            for part in which:
                for s in range(shard // 128):
                    for p in range(pack):
                        to = (p * parts + part) * rows
                        lhs[2 * k + other, to : to + rows, s * wide : (s + 1) * wide] = out[
                            at : at + rows, p * wide : (p + 1) * wide
                        ]
                    at += rows

    def multiply(layer, slots, first):
        for g in range(0, groups, 2):
            many = min(2, groups - g)
            total = None
            for k, other in slots:
                i = block_at(k, other)
                if pack == 1:
                    at = pl.ds(pl.multiple_of(i * shard, shard), shard)
                    weights = w[layer, at, g * hd : (g + many) * hd]
                else:
                    at = pl.ds(i * (shard // 8), shard // 8)
                    weights = jnp.concatenate(
                        [
                            w[layer, at, g + j].reshape(pack * shard, hd)
                            for j in range(many)
                        ],
                        axis=1,
                    )
                term = jnp.dot(lhs[2 * k + other], weights, preferred_element_type=F32)
                total = term if total is None else total + term
            cols = slice(g * hd, (g + many) * hd)
            acc[:, cols] = total if first else acc[:, cols] + total

    def project(layer):
        every, last = list(range(parts)), [parts - 1]
        home = [(0, 0), (0, 1)]
        direct = [(k, 0) for k in range(1, chips)]
        passed = [(k, 1) for k in range(1, chips)]
        squares[...] = jnp.zeros_like(squares)
        for part in every:
            arrive(xg.at[layer, part, 1, 0], ag_recv.at[1, layer, part])
        w_wait(layer, 0)
        expand(layer, home, every)
        multiply(layer, home, True)
        if layer + 1 < layers:
            for copy in w_copies(layer + 1):
                copy.start()
            for which in range(2):
                state_copy(which, layer + 1).start()
            wo_copy(layer + 1).start()
        for part in every[:-1]:
            forward(layer, part)
            expand(layer, direct, [part])
            forwarded(layer, part)
            expand(layer, passed, [part])
        forward(layer, parts - 1)
        expand(layer, direct, last)
        for k in range(1, chips):
            w_wait(layer, k)
        multiply(layer, direct, False)
        forwarded(layer, parts - 1)
        expand(layer, passed, last)
        multiply(layer, passed, False)
        total = jnp.concatenate([squares[part] for part in every], axis=0)
        return lax.rsqrt(jnp.sum(total, axis=-1, keepdims=True) / width + EPSILON)

    def norm(v):
        return v * lax.rsqrt(jnp.mean(v * v, axis=-1, keepdims=True) + EPSILON)

    def dots(a, b):
        return jnp.sum(a * b, axis=-1, keepdims=True)

    def tok(t):
        return slice(t * batch, (t + 1) * batch)

    def per_pair(fn, many):
        step = 4 if batch % 4 == 0 else 1

        def body(i, carry):
            for j in range(step):
                b = i * step + j
                for h in range(0, heads, many):
                    fn(b, list(range(h, min(h + many, heads))))
            return carry

        lax.fori_loop(0, batch // step, body, 0)

    def mesa(layer, factor):

        def projected(j, h):
            at = j * heads + h
            p, g = at % pack, at // pack
            return acc[p * full : (p + 1) * full, g * hd : (g + 1) * hd] * factor

        for h in range(heads):
            kq[h, full:, :] = norm(projected(0, h))
            kq[h, :full, :] = norm(projected(1, h)) * hd ** (-0.5)
            left_ref[layer, h, full:, :] = projected(2, h)
        state_copy(0, layer).wait()

        def first(b, hs):
            at = pl.ds(b, 2 * tokens, stride=batch)
            both = jnp.concatenate([kq[h, at, :] for h in hs], axis=0).astype(BF16)
            mats = jnp.concatenate([rv[layer, b, h].astype(BF16) for h in hs], axis=1)
            out = jnp.dot(both, mats, preferred_element_type=F32)
            for j, h in enumerate(hs):
                pz[h, at, :] = out[
                    j * 2 * tokens : (j + 1) * 2 * tokens, j * hd : (j + 1) * hd
                ]

        per_pair(first, 2)
        for h in range(heads):
            g = jnp.full((batch, 1), dec_ref[layer, h], F32)
            ginv = 1.0 / g
            ks = [kq[h, tok(t), :] for t in range(tokens)]
            qs = [kq[h, tok(tokens + t), :] for t in range(tokens)]
            ps = [pz[h, tok(t), :] for t in range(tokens)]
            zs = [pz[h, tok(tokens + t), :] for t in range(tokens)]
            back = [None] * (tokens + 1)
            front = [None] * (tokens + 1)
            back[0] = front[0] = jnp.ones_like(g)
            for t in range(tokens):
                back[t + 1] = back[t] * ginv
                front[t + 1] = front[t] * g
            for t in range(tokens):
                u = ps[t]
                inv = 1.0 / (g + dots(ks[t], u))
                for s in range(t + 1, tokens):
                    ps[s] = (ps[s] - u * (dots(u, ks[s]) * inv)) * ginv
                for s in range(t, tokens):
                    zs[s] = (zs[s] - u * (dots(u, qs[s]) * inv)) * ginv
                left_ref[layer, h, tok(t), :] = u
                right_ref[layer, h, tok(t), :] = u * (-inv * back[tokens - t])
                right_ref[layer, h, tok(tokens + t), :] = ks[t] * front[tokens - 1 - t]
                pz[h, tok(t), :] = zs[t]
        state_copy(1, layer).wait()

        def second(b, hs):
            at = pl.ds(b, 2 * tokens, stride=batch)
            both = jnp.concatenate([pz[h, at, :] for h in hs], axis=0).astype(BF16)
            mats = jnp.concatenate([sv[layer, b, h].astype(BF16) for h in hs], axis=0)
            out = lax.dot_general(
                both, mats, (((1,), (1,)), ((), ())), preferred_element_type=F32
            )
            for j, h in enumerate(hs):
                os[h, at, :] = out[
                    j * 2 * tokens : (j + 1) * 2 * tokens, j * hd : (j + 1) * hd
                ]

        per_pair(second, 2)
        for h in range(heads):
            g = jnp.full((batch, 1), dec_ref[layer, h], F32)
            front = [jnp.ones_like(g)]
            for t in range(tokens):
                front.append(front[-1] * g)
            outs = []
            for t in range(tokens):
                z = pz[h, tok(t), :]
                out = os[h, tok(t), :] * front[t + 1]
                for s in range(t + 1):
                    v = left_ref[layer, h, tok(tokens + s), :]
                    out = out + v * (dots(kq[h, tok(s), :], z) * front[t - s])
                outs.append(out)
            oo[:, h * hd : (h + 1) * hd] = jnp.concatenate(outs, axis=0).astype(BF16)

    def update(layer):
        upper = lax.broadcasted_iota(jnp.int32, (2 * tokens, hd), 0) < tokens
        scales = []
        for h in range(heads):
            g = jnp.full((1, hd), dec_ref[layer, h], F32)
            power = g
            for _ in range(tokens - 1):
                power = power * g
            scales.append((power, 1.0 / power))

        def change_of(b, hs):
            h = hs[0]
            at = pl.ds(b, 2 * tokens, stride=batch)
            left = left_ref[layer, h, at, :]
            right = right_ref[layer, h, at, :]
            zero = jnp.zeros_like(right)
            both = jnp.concatenate(
                [jnp.where(upper, right, zero), jnp.where(upper, zero, right)], axis=1
            ).astype(BF16)
            change = jnp.dot(left.T.astype(BF16), both, preferred_element_type=F32)
            rv[layer, b, h] = rv[layer, b, h] * scales[h][1] + change[:, :hd]
            sv[layer, b, h] = sv[layer, b, h] * scales[h][0] + change[:, hd:]

        per_pair(change_of, 1)

    def mix(layer):
        def product(k, other):
            i = 2 * lax.rem(chip + k, chips) + (1 - side if other else side)
            col = pl.ds(pl.multiple_of(i * shard, shard), shard)
            return jnp.dot(oo[...], wo[layer, :, col], preferred_element_type=F32)

        order = list(range(1, chips)) + [0]
        for k in order:
            out = product(k, 1).astype(BF16)
            for part in range(parts):
                near[layer, part, k] = out[part * rows : (part + 1) * rows]
        for part in range(parts):
            for k in order:
                send(
                    layer, 2, near.at[layer, part, k], far.at[layer, part, k],
                    rs_recv.at[0, layer, part], sibling,
                )
        for k in order:
            out = product(k, 0)
            for part in range(parts):
                mine[part, k] = out[part * rows : (part + 1) * rows]

    def scatter(layer, part):
        arrive(far.at[layer, part], rs_recv.at[0, layer, part])
        for k in range(1, chips):
            pair[layer, part, k] = (
                mine[part, k] + far[layer, part, k].astype(F32)
            ).astype(BF16)
            send(
                layer, 3, pair.at[layer, part, k], recv.at[layer, part, k],
                rs_recv.at[1, layer, part], peer(k),
            )

    def collect(layer, part):
        total = cur[part] + mine[part, 0] + far[layer, part, 0].astype(F32)
        arrive(recv.at[layer, part, pl.ds(1, chips - 1)], rs_recv.at[1, layer, part])
        for k in range(1, chips):
            total = total + recv[layer, part, k].astype(F32)
        cur[part] = total
        if layer + 1 < layers:
            xg[layer + 1, part, 0, 0] = total.astype(BF16)
            gather_start(layer + 1, part)
        else:
            y_ref[part * rows : (part + 1) * rows, :] = total

    every = range(parts)
    for part in every:
        gather_start(0, part)
    for copy in misc[1:]:
        copy.wait()
    state_copy(0, 0).start()
    state_copy(1, 0).start()
    wo_copy(0).start()
    for layer in range(layers):
        factor = project(layer)
        mesa(layer, factor)
        wo_copy(layer).wait()
        mix(layer)
        for part in every:
            scatter(layer, part)
        if layer + 1 < layers:
            update(layer)
            for part in every:
                collect(layer, part)
        else:
            update(layer)
            for at in range(layers - 1):
                settle(at)
            for part in every:
                collect(layer, part)
    settle(layers - 1)


def back_kernel(y_vmem, s_vmem, r_vmem, y_hbm, s_hbm, r_hbm, sems):
    whole = []
    for i, (src, dst) in enumerate(((s_vmem, s_hbm), (r_vmem, r_hbm), (y_vmem, y_hbm))):
        whole.append(pltpu.make_async_copy(src, dst, sems.at[i]))
        if i == 2:
            whole[i].start()
            continue
        cut = src.shape[1] // CUTS
        for layer in range(src.shape[0]):
            for c in range(CUTS):
                at = (layer, pl.ds(c * cut, cut))
                pltpu.make_async_copy(src.at[at], dst.at[at], sems.at[i]).start()
    for copy in whole:
        copy.wait()


def on_device(n, inputs, gains, decays, w_qkv, w_out, s_state, r_state):
    layers, width, _, heads, hd = w_qkv.shape
    tokens, batch, shard = inputs.shape
    full = tokens * batch
    parts = PARTS if full % (16 * PARTS) == 0 else 1
    rows = full // parts
    mixed = 3 * heads
    pack = 2 if heads % 2 == 0 else 1
    groups = mixed // pack
    chips = n // 2
    vmem = pl.BlockSpec(memory_space=pltpu.VMEM)
    anywhere = pl.BlockSpec(memory_space=pl.ANY)
    if pack == 1:
        w_view = w_qkv.reshape(layers, width, mixed * hd)
        w_vmem = pltpu.VMEM(w_view.shape, BF16)
    else:
        w_view = w_qkv.reshape(layers, width // 8, 8, groups, pack, hd)
        w_vmem = pltpu.VMEM((layers, width // 8, groups, 8 * pack, hd), BF16)
    blocks = (layers, parts, chips, rows, shard)
    pairs = (layers, heads, 2 * full, hd)
    dma = pltpu.SemaphoreType.DMA
    y, s_new, r_new = pl.pallas_call(
        functools.partial(front_kernel, n, tokens, batch, heads, layers, parts),
        out_shape=(
            pltpu.VMEM((full, shard), F32),
            pltpu.VMEM(s_state.shape, F32),
            pltpu.VMEM(r_state.shape, F32),
        ),
        in_specs=[anywhere] * 7,
        out_specs=(vmem, vmem, vmem),
        scratch_shapes=[
            pltpu.VMEM(inputs.shape, BF16),
            pltpu.VMEM((layers, width), F32),
            pltpu.SMEM(decays.shape, F32),
            w_vmem,
            pltpu.VMEM((layers, heads * hd, width), BF16),
            pltpu.VMEM((128, 128 * pack * 2), BF16),
            pltpu.VMEM((layers, parts, 2, chips, rows, shard), BF16),
            pltpu.VMEM((n, pack * full, pack * shard), BF16),
            pltpu.VMEM((pack * full, groups * hd), F32),
            pltpu.VMEM((parts, rows, 128), F32),
            pltpu.VMEM(blocks, BF16),
            pltpu.VMEM(blocks, BF16),
            pltpu.VMEM(blocks, BF16),
            pltpu.VMEM(blocks, BF16),
            pltpu.VMEM(blocks[1:], F32),
            pltpu.VMEM((parts, rows, shard), F32),
            pltpu.VMEM((heads, 2 * full, hd), F32),
            pltpu.VMEM((heads, 2 * full, hd), F32),
            pltpu.VMEM((heads, 2 * full, hd), F32),
            pltpu.VMEM((full, heads * hd), BF16),
            pltpu.VMEM(pairs, F32),
            pltpu.VMEM(pairs, F32),
            dma((3,)),
            dma((layers, chips)),
            dma((layers,)),
            dma((2, layers)),
            dma((layers, 4)),
            dma((3, layers, parts)),
            dma((2, layers, parts)),
        ],
        compiler_params=pltpu.CompilerParams(
            collective_id=0, has_side_effects=True, vmem_limit_bytes=44 * 1024 * 1024
        ),
        name="front",
    )(
        inputs,
        gains,
        decays,
        w_view,
        w_out.reshape(layers, heads * hd, width),
        s_state,
        r_state,
    )
    out = pl.pallas_call(
        back_kernel,
        out_shape=tuple(jax.ShapeDtypeStruct(a.shape, F32) for a in (y, s_state, r_state)),
        in_specs=[vmem] * 3,
        out_specs=(anywhere,) * 3,
        scratch_shapes=[dma((3,))],
        compiler_params=pltpu.CompilerParams(vmem_limit_bytes=1024 * 1024),
        name="back",
    )(y, s_new, r_new)
    return out[0].reshape(inputs.shape), out[1], out[2]


def solution(mesh):
    in_specs = (
        P(None, "grp", "head"),
        P(),
        P(None, "head"),
        P(None, None, None, "head", None),
        P(None, "head", None, None),
        P(None, "grp", "head", None, None),
        P(None, "grp", "head", None, None),
    )
    out_specs = (
        P(None, "grp", "head"),
        P(None, "grp", "head", None, None),
        P(None, "grp", "head", None, None),
    )
    return jax.shard_map(
        functools.partial(on_device, mesh.shape["head"]),
        mesh=mesh,
        in_specs=in_specs,
        out_specs=out_specs,
        check_vma=False,
    )
```

time: 47.3 us -> 43.3 us (0.915)
  Pallas kernels: 46.5 us -> 42.5 us
    pallas_call x1, Pallas kernels: 40.4 us -> 36.7 us  [on_device(): pl.pallas_call(functools.partial(front_kernel, n, tokens, batch, heads, l...]
where the time goes in v2:
time: 43.3 us; the launch traced here: 43.2 us
  Pallas kernels  42.5 us (98%)
  between operations  0.64 us (1%)
    pallas_call x1, Pallas kernels, on_device(): pl.pallas_call(functools.partial(front_kernel, n, tokens, batch, heads, l...  36.7 us
    pallas_call x1, Pallas kernels, on_device(): pl.pallas_call(back_kernel, out_shape=tuple((jax.ShapeDtypeStruct(a.shape...  5.85 us

profile of v2, /device:TPU:0, one launch (start us, length us, event | category | flops | bytes accessed | tf_op | source)
XLA Modules:
  0.0 43.2 jit_solution(16688911565233711554)
XLA Ops:
  0.6 36.7 %front.1 = (f32[64,512]{1,0:T(8,128)S(1)}, f32[2,16,4,128,128]{4,3,2,1,0:T(8,128)S(1)}, f32[2,16,4,128,128]{4,3,2,1,0:T(8,128)S(1)}) custom-call(bf16[4,16,512]{2,1,0:T(8,128)(2,1)} %x_hbm.1, f32[2,4096]{1,0:T(2,128)} %gains_hbm.1, f32[2,4]{1,0:T(2,128)} %dec_hbm.1, bf16[2,512,8,6,2,128]{5,4,3,2,1,0:T(2,128)(2,1)} %bitcast.3, bf16[2,512,4096]{2,1,0:T(8,128)(2,1)} %bitcast.4, ...), custom_call_target="tpu_custom_call" | custom-call | tf_op jit(solution)/shard_map/front/pallas_call | solution.py:472
  37.3 5.8 %back.1 = (f32[64,512]{1,0:T(8,128)}, f32[2,16,4,128,128]{4,3,2,1,0:T(8,128)}, f32[2,16,4,128,128]{4,3,2,1,0:T(8,128)}) custom-call(f32[64,512]{1,0:T(8,128)S(1)} %get-tuple-element.9.y_vmem, f32[2,16,4,128,128]{4,3,2,1,0:T(8,128)S(1)} %get-tuple-element.10.s_vmem, f32[2,16,4,128,128]{4,3,2,1,0:T(8,128)S(1)} %get-tuple-element.11.r_vmem), custom_call_target="tpu_custom_call" | custom-call | tf_op jit(solution)/shard_map/back/pallas_call | solution.py:525

commit v3 on v2

--- a/solution.py
+++ b/solution.py
@@ -204,12 +204,10 @@
 
     def project(layer):
         every, last = list(range(parts)), [parts - 1]
-        home = [(0, 0), (0, 1)]
+        home, beside = [(0, 0)], [(0, 1)]
         direct = [(k, 0) for k in range(1, chips)]
         passed = [(k, 1) for k in range(1, chips)]
         squares[...] = jnp.zeros_like(squares)
-        for part in every:
-            arrive(xg.at[layer, part, 1, 0], ag_recv.at[1, layer, part])
         w_wait(layer, 0)
         expand(layer, home, every)
         multiply(layer, home, True)
@@ -222,13 +220,17 @@
         for part in every[:-1]:
             forward(layer, part)
             expand(layer, direct, [part])
+        for part in every:
+            arrive(xg.at[layer, part, 1, 0], ag_recv.at[1, layer, part])
+        expand(layer, beside, every)
+        for part in every[:-1]:
             forwarded(layer, part)
             expand(layer, passed, [part])
         forward(layer, parts - 1)
         expand(layer, direct, last)
         for k in range(1, chips):
             w_wait(layer, k)
-        multiply(layer, direct, False)
+        multiply(layer, beside + direct, False)
         forwarded(layer, parts - 1)
         expand(layer, passed, last)
         multiply(layer, passed, False)
@@ -245,7 +247,7 @@
         return slice(t * batch, (t + 1) * batch)
 
     def per_pair(fn, many):
-        step = 4 if batch % 4 == 0 else 1
+        step = 4 * many if batch % (4 * many) == 0 else 1
 
         def body(i, carry):
             for j in range(step):

time: 43.3 us -> 42.4 us (0.979)
  Pallas kernels: 42.5 us -> 41.6 us
    pallas_call x1, Pallas kernels: 36.7 us -> 35.8 us  [on_device(): pl.pallas_call(functools.partial(front_kernel, n, tokens, batch, heads, l...]
where the time goes in v3:
time: 42.4 us; the launch traced here: 42.2 us
  Pallas kernels  41.6 us (98%)
  between operations  0.64 us (2%)
    pallas_call x1, Pallas kernels, on_device(): pl.pallas_call(functools.partial(front_kernel, n, tokens, batch, heads, l...  35.8 us
    pallas_call x1, Pallas kernels, on_device(): pl.pallas_call(back_kernel, out_shape=tuple((jax.ShapeDtypeStruct(a.shape...  5.85 us

profile of v3, /device:TPU:0, one launch (start us, length us, event | category | flops | bytes accessed | tf_op | source)
XLA Modules:
  0.0 42.2 jit_solution(9255990654676519457)
XLA Ops:
  0.6 35.8 %front.1 = (f32[64,512]{1,0:T(8,128)S(1)}, f32[2,16,4,128,128]{4,3,2,1,0:T(8,128)S(1)}, f32[2,16,4,128,128]{4,3,2,1,0:T(8,128)S(1)}) custom-call(bf16[4,16,512]{2,1,0:T(8,128)(2,1)} %x_hbm.1, f32[2,4096]{1,0:T(2,128)} %gains_hbm.1, f32[2,4]{1,0:T(2,128)} %dec_hbm.1, bf16[2,512,8,6,2,128]{5,4,3,2,1,0:T(2,128)(2,1)} %bitcast.3, bf16[2,512,4096]{2,1,0:T(8,128)(2,1)} %bitcast.4, ...), custom_call_target="tpu_custom_call" | custom-call | tf_op jit(solution)/shard_map/front/pallas_call | solution.py:474
  36.4 5.8 %back.1 = (f32[64,512]{1,0:T(8,128)}, f32[2,16,4,128,128]{4,3,2,1,0:T(8,128)}, f32[2,16,4,128,128]{4,3,2,1,0:T(8,128)}) custom-call(f32[64,512]{1,0:T(8,128)S(1)} %get-tuple-element.9.y_vmem, f32[2,16,4,128,128]{4,3,2,1,0:T(8,128)S(1)} %get-tuple-element.10.s_vmem, f32[2,16,4,128,128]{4,3,2,1,0:T(8,128)S(1)} %get-tuple-element.11.r_vmem), custom_call_target="tpu_custom_call" | custom-call | tf_op jit(solution)/shard_map/back/pallas_call | solution.py:527
